TPU v7x, 32 devices: a whole 2x2x4 slice. The times are simulated.
32 devices in a mesh: ctx: 8 (over z, y), req: 4 (over x, core).
Axes of the slice: x: 2, y: 2, z: 4, core: 2. Of those that a mesh axis runs over, the one named last changes fastest.
Arguments:
- queries: bfloat16 [4096, 1024], P(('req', 'ctx')), parts along dimension 0, may hold values from -6 to 6
- keys: bfloat16 [4096, 256], P(('req', 'ctx')), parts along dimension 0, may hold values from -6 to 6
- lse: float32 [16, 4096], P(None, ('req', 'ctx')), parts along dimension 1, may hold values from -0.5 to 15, as said below
- length: int32 [4], P('req'), parts along dimension 0, may hold values from 512 to 1024
Outputs:
- key_scores: float32 [16, 4096], P(None, ('req', 'ctx')), parts along dimension 1
There are 4 independent parts, one for each index of `req`. A program takes and returns all parts, laid end to end along the dimension named above; each array names one. Nothing has to cross between parts.
Inputs may be any that keep to these rules, and one draw needn't show every extreme that they name: lse[h, i] is the logarithm of i + 1 plus an offset between -0.5 and 3.
All inputs are finite; a program needn't handle non-finite values.
Results may differ from a plain program's by a relative error of at most 0.0003.
Values may be sent and summed in bfloat16 or wider, within the bound.
No kernel may reach another device: no remote copies, remote signals or barrier semaphores. Data moves between devices by JAX's collectives and lax.ppermute only.
A program may use at most 64 MiB of HBM per device.

v0:
```python
import math
import jax
import jax.numpy as jnp
from jax import lax
from jax.sharding import PartitionSpec as P

HEAD_DIM = 64


def block_terms(query_set, lse_set, positions, key_block, key_start, limit):
    heads = lse_set.shape[0]
    rows_here = query_set.shape[0]
    width = key_block.shape[0]
    kv_heads = key_block.shape[1] // HEAD_DIM
    grouped = query_set.reshape(rows_here, kv_heads, heads // kv_heads, HEAD_DIM)
    key_view = key_block.reshape(width, kv_heads, HEAD_DIM)
    logits = jnp.einsum("rhgd,chd->hgrc", grouped, key_view, preferred_element_type=jnp.float32)
    logits = logits.reshape(heads, rows_here, width) * HEAD_DIM ** (-0.5)
    key_pos = key_start + jnp.arange(width, dtype=jnp.int32)
    valid = (positions[:, None] >= key_pos[None, :]) & (positions[:, None] < limit)
    weights = jnp.where(valid[None], jnp.exp(logits - lse_set[:, :, None]), jnp.float32(0.0))
    return jnp.sum(weights, axis=1)


def make_absorb(query_sets, limit, heads, total, piece, start):
    width = piece.shape[0]
    step_len = math.gcd(width, 512)
    turns = width // step_len

    def skipped(*operands):
        return jnp.zeros((heads, step_len), jnp.float32)

    def one_turn(turn, running):
        offset = turn * step_len
        key_block = lax.dynamic_slice_in_dim(piece, offset, step_len, 0)
        key_start = start + offset
        part_sum = jnp.zeros((heads, step_len), jnp.float32)
        for query_set, lse_set, positions in query_sets:
            needed = (key_start <= jnp.max(positions)) & (key_start < limit)
            part_sum = lax.cond(
                needed,
                block_terms,
                skipped,
                query_set,
                lse_set,
                positions,
                key_block,
                key_start,
                limit,
            )
        current = lax.dynamic_slice(running, (0, key_start), (heads, step_len))
        return lax.dynamic_update_slice(running, current + part_sum, (0, key_start))

    return lax.fori_loop(0, turns, one_turn, total)


def shards(queries, keys, lse, length):
    tok_rows = queries.shape[0]
    heads = lse.shape[0]
    devices_ctx = lax.axis_size("ctx")
    my_index = lax.axis_index("ctx")
    limit = length[0]
    first_row = my_index * tok_rows
    query_sets = [(queries, lse, first_row + jnp.arange(tok_rows, dtype=jnp.int32))]
    empty = jnp.zeros((heads, tok_rows * devices_ctx), jnp.float32)
    totals = make_absorb(
        query_sets,
        limit,
        heads,
        empty,
        lax.all_gather(keys, "ctx", axis=0, tiled=True),
        jnp.int32(0),
    )
    return lax.psum_scatter(totals, "ctx", scatter_dimension=1, tiled=True)


def solution(mesh):
    placed = (P(("req", "ctx"), None), P(("req", "ctx"), None), P(None, ("req", "ctx")), P("req"))
    return jax.shard_map(
        shards, mesh=mesh, in_specs=placed, out_specs=P(None, ("req", "ctx")), check_vma=False
    )
```

profile of v0, /device:TPU:0, one launch (start us, length us, event | category | flops | bytes accessed | tf_op | source)
XLA Modules:
  0.0 107.6 jit_solution(11371074071570174559)
XLA Ops:
  6.5 0.0 reduce-scatter.2.cloned.1.call-start
  6.5 0.7 add_reduce_fusion
  7.2 0.9 copy.5
  8.2 0.0 copy-start.1
  8.2 1.1 %copy.6 = bf16[128,1024]{0,1:T(8,128)(2,1)S(1)} copy(bf16[128,1024]{1,0:T(8,128)(2,1)} %param.8) | data formatting | bytes 524288
  9.3 29.6 %all_gather.3 = bf16[1024,256]{0,1:T(8,128)(2,1)S(1)} all-gather(bf16[128,256]{0,1:T(8,128)(2,1)S(1)} %copy.5), channel_id=1, replica_groups=mesh['ctx'=8,'req'=4] {'ctx'}, dimensions={0}, use_global_device_ids=true | all-gather | bytes 589824 | tf_op jit(solution)/shard_map/all_gather | solution.py:71
  38.9 0.0 copy-done.1
  38.9 4.9 %while.15 = (s32[]{:T(128)}, f32[16,1024]{1,0:T(8,128)S(1)}, s32[]{:T(128)}, s32[]{:T(128)}, bf16[1024,256]{0,1:T(8,128)(2,1)S(1)}, /*index=5*/bf16[128,1024]{0,...) while((s32[]{:T(128)}, f32[16,1024]{1,0:T(8,128)S(1)}, ...), condition=%wide.region_5.6_spmd.clone, body=%wide.region_1.5_spmd.clone.sunk | while | flops 138543888 | bytes 1391129 | solution.py:54
  40.2 2.2 %conditional.3 = (f32[16,512]{1,0:T(8,128)S(1)}) conditional(s32[]{:T(128)} %convert_element_type.10, () %tuple.49, (s32[]{:T(128)}, s32[]{:T(128)}, s32[]{:T(128)}, bf16[1024,256]{0,1:T(8,128)(2,1)S(1)}, s32[]{:T(128)}, /*index=5*/bf16[128,1024]{0,1:T(8,128)(2,1)S(1)}, f32[16,128]{1,0:T(8,128)S(1)}, s32[128]{0:T(128)S(1)}) %tuple.50), branch_computations={%region_2.0_spmd, %region_3.4_spmd} | conditional | flops 138535680 | bytes 1292056 | solution.py:40
  40.2 0.7 broadcast_compare_fusion
  40.9 0.1 compare_and_fusion
  41.0 1.4 %fusion.4 = f32[4,4,512]{2,1,0:T(4,128)S(1)} fusion(bf16[512,4,64,1]{0,2,3,1:T(8,128)(2,1)S(1)} %bitcast.18, bf16[128,4,4,64]{0,3,2,1:T(8,128)(2,1)S(1)} %bitcast.19, f32[4,4,128]{2,1,0:T(4,128)S(1)} %bitcast.20, pred[128,512]{1,0:T(8,128)(4,1)S(1)} %compare_and_fusion), kind=kOutput, calls=%fused_computation.4 | convolution fusion | flops 138403840 | bytes 630784 | tf_op jit(solution)/shard_map/while/body/eval_jaxpr/cond/branch_1_fun/rhgd,chd->hgrc/dot_general | solution.py:17
  43.8 0.0 copy-start
  43.8 0.6 copy-done
  44.4 0.0 reduce-scatter.2.cloned.1.call-update
  44.5 56.3 %reduce-scatter.2.cloned.1.call-done = f32[16,128]{1,0:T(8,128)} async-done(((f32[16,1024]{1,0:T(8,128)}), f32[16,128]{1,0:T(8,128)}) %reduce-scatter.2.cloned.1.call-update) | async-done | bytes 8208 | tf_op jit(solution)/shard_map/reduce_scatter | solution.py:74
  (10 shorter events, 0.1 us)
Async XLA Ops:
  6.5 94.3 %reduce-scatter.2.cloned.1.call-start = ((), (), s32[]{:S(2)}) async-start(), calls=%async_computation.1 | async-start | bytes 73728 | tf_op jit(solution)/shard_map/reduce_scatter | solution.py:74
  8.2 30.7 %copy-start.1 = (f32[16,128]{1,0:T(8,128)S(1)}, f32[16,128]{1,0:T(8,128)}, u32[]{:S(2)}) copy-start(f32[16,128]{1,0:T(8,128)} %param.10) | copy-start | bytes 24580
  43.8 0.6 copy-start
Sparse Core Ops, SparseCore 0:
  44.6 56.1 reduce-scatter.1
where the time goes:
time: 108 us
  waiting for transfers between devices  56.3 us (52%)
  blocking collectives  29.6 us (27%)
  between operations  13.4 us (12%)
  local copies, waits for them, and re-layouts  2.75 us (3%)
  loops' own time  2.73 us (3%)
  other arithmetic  1.46 us (1%)
  matrix products  1.35 us (1%)
    reduce_scatter x1, waiting for transfers between devices, shards(): return lax.psum_scatter(totals, 'ctx', scatter_dimension=1, tiled=True)  56.3 us
    all_gather x1, blocking collectives, shards(): lax.all_gather(keys, 'ctx', axis=0, tiled=True)  29.6 us
    unnamed x6, local copies, waits for them, and re-layouts  2.69 us
    another operation x1, loops' own time, make_absorb(): return lax.fori_loop(0, turns, one_turn, total)  2.66 us
  transfers between devices with their start and end apart: 1, of which 1 were waited for; matrix products, arithmetic and copies ran while one was open for 0% of the time, Pallas kernels for 0%

commit v1 on v0

--- a/solution.py
+++ b/solution.py
@@ -68,7 +68,9 @@
         limit,
         heads,
         empty,
-        lax.all_gather(keys, "ctx", axis=0, tiled=True),
+        jnp.concatenate(
+            lax.all_to_all(jnp.stack([keys] * lax.axis_size("ctx")), "ctx", 0, 0), axis=0
+        ),
         jnp.int32(0),
     )
     return lax.psum_scatter(totals, "ctx", scatter_dimension=1, tiled=True)

time: 108 us -> 100 us (0.926)
  blocking collectives: 29.6 us -> 0 us
  waiting for transfers between devices: 56.3 us -> 69.7 us
  starting transfers between devices: 0.01 us -> 7.48 us
    all_gather x1 -> x0, blocking collectives: 29.6 us -> none  [shards(): lax.all_gather(keys, 'ctx', axis=0, tiled=True)]
    all_to_all x0 -> x1, waiting for transfers between devices: none -> 13.6 us  [shards(): lax.all_to_all(jnp.stack([keys] * lax.axis_size('ctx')), 'ctx', 0, 0)]
    all_to_all x0 -> x1, starting transfers between devices: none -> 7.44 us  [shards(): lax.all_to_all(jnp.stack([keys] * lax.axis_size('ctx')), 'ctx', 0, 0)]
    unnamed x6 -> x9, local copies, waits for them, and re-layouts: 2.69 us -> 2.4 us
  transfers between devices with their start and end apart: 1 -> 2, of which waited for: 1 -> 2; matrix products, arithmetic and copies ran while one was open for 0% -> 1% of each run, Pallas kernels for 0% -> 0%
where the time goes in v1:
time: 100 us; the launch traced here: 99.8 us
  waiting for transfers between devices  69.7 us (70%)
  between operations  13.5 us (14%)
  starting transfers between devices  7.48 us (7%)
  local copies, waits for them, and re-layouts  3.53 us (4%)
  loops' own time  2.79 us (3%)
  other arithmetic  1.49 us (1%)
  matrix products  1.34 us (1%)
    reduce_scatter x1, waiting for transfers between devices, shards(): return lax.psum_scatter(totals, 'ctx', scatter_dimension=1, tiled=True)  56.1 us
    all_to_all x1, waiting for transfers between devices, shards(): lax.all_to_all(jnp.stack([keys] * lax.axis_size('ctx')), 'ctx', 0, 0)  13.6 us
    all_to_all x1, starting transfers between devices, shards(): lax.all_to_all(jnp.stack([keys] * lax.axis_size('ctx')), 'ctx', 0, 0)  7.44 us
    another operation x1, loops' own time, make_absorb(): return lax.fori_loop(0, turns, one_turn, total)  2.71 us
    unnamed x9, local copies, waits for them, and re-layouts  2.4 us
  transfers between devices with their start and end apart: 2, of which 2 were waited for; matrix products, arithmetic and copies ran while one was open for 1% of the time, Pallas kernels for 0%

profile of v1, /device:TPU:0, one launch (start us, length us, event | category | flops | bytes accessed | tf_op | source)
XLA Modules:
  0.0 99.8 jit_solution(1489892444329969358)
XLA Ops:
  6.5 0.9 copy.9
  7.5 0.9 stack.2
  8.4 0.0 copy-start.1
  8.4 7.4 %all-to-all-start = ((bf16[8,128,256]{1,2,0:T(8,128)(2,1)}), bf16[8,128,256]{1,2,0:T(8,128)(2,1)S(1)}, u32[]{:S(2)}, u32[]{:S(2)}) async-start(bf16[8,128,256]{1,2,0:T(8,128)(2,1)} %stack.2), calls=%async_computation | async-start | bytes 1048576 | tf_op jit(solution)/shard_map/all_to_all | solution.py:72
  15.8 0.0 reduce-scatter.2.cloned.1.call-start
  15.8 0.7 add_reduce_fusion
  16.5 0.0 copy-done.1
  16.5 0.2 copy.12
  16.7 13.6 %all-to-all-done = bf16[8,128,256]{1,2,0:T(8,128)(2,1)S(1)} async-done(((bf16[8,128,256]{1,2,0:T(8,128)(2,1)}), bf16[8,128,256]{1,2,0:T(8,128)(2,1)S(1)}, u32[]{:S(2)}, u32[]{:S(2)}) %all-to-all-start) | async-done | bytes 524320 | tf_op jit(solution)/shard_map/all_to_all | solution.py:72
  30.3 0.2 copy.10
  30.5 0.0 copy-start.2
  30.5 0.2 copy.11
  30.7 0.5 copy-done.2
  31.2 5.0 %while.15 = (s32[]{:T(128)}, f32[16,1024]{1,0:T(8,128)S(1)}, s32[]{:T(128)}, s32[]{:T(128)}, bf16[1024,256]{0,1:T(8,128)(2,1)S(1)}, /*index=5*/bf16[128,1024]{0,...) while((s32[]{:T(128)}, f32[16,1024]{1,0:T(8,128)S(1)}, ...), condition=%wide.region_5.6_spmd.clone, body=%wide.region_1.5_spmd.clone.sunk | while | flops 138543888 | bytes 1391129 | solution.py:54
  32.5 2.2 %conditional.3 = (f32[16,512]{1,0:T(8,128)S(1)}) conditional(s32[]{:T(128)} %convert_element_type.10, () %tuple.51, (s32[]{:T(128)}, s32[]{:T(128)}, s32[]{:T(128)}, bf16[1024,256]{0,1:T(8,128)(2,1)S(1)}, s32[]{:T(128)}, /*index=5*/bf16[128,1024]{0,1:T(8,128)(2,1)S(1)}, f32[16,128]{1,0:T(8,128)S(1)}, s32[128]{0:T(128)S(1)}) %tuple.52), branch_computations={%region_2.0_spmd, %region_3.4_spmd} | conditional | flops 138535680 | bytes 1292056 | solution.py:40
  32.6 0.7 broadcast_compare_fusion
  33.2 0.1 compare_and_fusion
  33.4 1.3 %fusion.4 = f32[4,4,512]{2,1,0:T(4,128)S(1)} fusion(bf16[512,4,64,1]{0,2,3,1:T(8,128)(2,1)S(1)} %bitcast.19, bf16[128,4,4,64]{0,3,2,1:T(8,128)(2,1)S(1)} %bitcast.21, f32[4,4,128]{2,1,0:T(4,128)S(1)} %bitcast.22, pred[128,512]{1,0:T(8,128)(4,1)S(1)} %compare_and_fusion), kind=kOutput, calls=%fused_computation.4 | convolution fusion | flops 138403840 | bytes 630784 | tf_op jit(solution)/shard_map/while/body/eval_jaxpr/cond/branch_1_fun/rhgd,chd->hgrc/dot_general | solution.py:17
  36.2 0.0 copy-start
  36.2 0.6 copy-done
  36.8 0.0 reduce-scatter.2.cloned.1.call-update
  36.8 56.1 %reduce-scatter.2.cloned.1.call-done = f32[16,128]{1,0:T(8,128)} async-done(((f32[16,1024]{1,0:T(8,128)}), f32[16,128]{1,0:T(8,128)}) %reduce-scatter.2.cloned.1.call-update) | async-done | bytes 8208 | tf_op jit(solution)/shard_map/reduce_scatter | solution.py:76
  (10 shorter events, 0.1 us)
Async XLA Ops:
  8.4 8.2 %copy-start.1 = (bf16[128,1024]{1,0:T(8,128)(2,1)S(1)}, bf16[128,1024]{1,0:T(8,128)(2,1)}, u32[]{:S(2)}) copy-start(bf16[128,1024]{1,0:T(8,128)(2,1)} %param.8) | copy-start | bytes 786436
  8.4 21.9 %all-to-all-start = ((bf16[8,128,256]{1,2,0:T(8,128)(2,1)}), bf16[8,128,256]{1,2,0:T(8,128)(2,1)S(1)}, u32[]{:S(2)}, u32[]{:S(2)}) async-start(bf16[8,128,256]{1,2,0:T(8,128)(2,1)} %stack.2), calls=%async_computation | async-start | bytes 1048576 | tf_op jit(solution)/shard_map/all_to_all | solution.py:72
  15.8 77.2 %reduce-scatter.2.cloned.1.call-start = ((), (), s32[]{:S(2)}) async-start(), calls=%async_computation.2 | async-start | bytes 73728 | tf_op jit(solution)/shard_map/reduce_scatter | solution.py:76
  30.5 0.7 copy-start.2
  36.2 0.6 copy-start
Sparse Core Ops, SparseCore 0:
  37.0 55.9 reduce-scatter.1
